TPU v7x, 256 devices: a whole 4x4x8 slice. The times are simulated.
256 devices in a mesh: rows: 16 (over y, x_lo, core), cols: 4 (over z_1, x_hi), slabs: 2 (over z_0), trial: 2 (over z_2).
Axes of the slice: x: 4 (x_hi: 2, x_lo: 2; x = x_hi * 2 + x_lo), y: 4, z: 8 (z_0: 2, z_1: 2, z_2: 2; z = z_0 * 4 + z_1 * 2 + z_2), core: 2. Of those that a mesh axis runs over, the one named last changes fastest.
Arguments:
- field_values: float32 [256, 64, 128, 128], P(('trial', 'rows'), 'cols', 'slabs'), parts along dimension 0, may hold values from 0.2 to 1.8
- crowding: float32 [256, 64, 128, 128], P(('trial', 'rows'), 'cols', 'slabs'), parts along dimension 0, may hold values from 0.5 to 2
Outputs:
- potential: float32 [256, 64, 128, 128], P(('trial', 'rows'), 'cols', 'slabs'), parts along dimension 0
- field_values_end: float32 [256, 64, 128, 128], P(('trial', 'rows'), 'cols', 'slabs'), parts along dimension 0
There are 2 independent parts, one for each index of `trial`. A program takes and returns all parts, laid end to end along the dimension named above; each array names one. Nothing has to cross between parts.
All inputs are finite; a program needn't handle non-finite values.
Results may differ from a plain program's by a relative error of at most 0.00002.
Values sent between devices are 32-bit elements; how exact they have to be, the bound alone decides.
A program may use at most 64 MiB of HBM per device.

v0:
```python
import jax
import jax.numpy as jnp
from jax import lax
from jax.sharding import PartitionSpec as P

STEPS = 3


def with_halo(shard, sides, width):
    edges = {}
    for axis, dim in sides:
        devices, length = (lax.axis_size(axis), shard.shape[dim])
        up = [(i, (i + 1) % devices) for i in range(devices - 1)]
        last = lax.slice_in_dim(shard, length - width, length, axis=dim)
        initial = lax.slice_in_dim(shard, 0, width, axis=dim)
        edges[dim] = (
            lax.ppermute(last, axis, up),
            lax.ppermute(initial, axis, [(b, a) for a, b in up]),
        )
    done = []
    for _, dim in sides:
        low, high = edges[dim]
        around = [(width, width) if d in done else (0, 0) for d in range(shard.ndim)]
        shard = jnp.concatenate([jnp.pad(low, around), shard, jnp.pad(high, around)], axis=dim)
        done.append(dim)
    return shard


def entering(part, axis, combine, identity):
    place = lax.axis_index(axis)
    gathered = lax.all_gather(part, axis)
    state = jnp.zeros_like(part) + jnp.asarray(identity, part.dtype)

    def one(lap, state):
        return combine(state, lax.dynamic_index_in_dim(gathered, lap, 0, False))

    return lax.fori_loop(0, place, one, state)


def without_rim(values, dims):
    for dim in dims:
        values = lax.slice_in_dim(values, 1, values.shape[dim] - 1, axis=dim)
    return values


def shifted_cells(values, dim, start, dims):
    others = [other for other in dims if other != dim]
    values = without_rim(values, others)
    return lax.slice_in_dim(values, start, start + values.shape[dim] - 2, axis=dim)


def march_step(padded, crowding):
    middle = without_rim(padded, (0, 1, 2))
    lower = [shifted_cells(padded, dim, 0, (0, 1, 2)) for dim in (0, 1, 2)]
    upper = [shifted_cells(padded, dim, 2, (0, 1, 2)) for dim in (0, 1, 2)]
    spread = lower[0] + upper[0] + lower[1] + upper[1] + lower[2] + upper[2] - 6.0 * middle
    return middle + 0.1 * spread + 0.2 * middle * (1.0 - middle * crowding)


def on_device(field_values, crowding):
    for step in range(STEPS):
        padded = with_halo(field_values, (("rows", 0), ("cols", 1), ("slabs", 2)), 1)
        field_values = march_step(padded, crowding)
    here = jnp.cumsum(field_values, axis=0)
    total = lax.slice_in_dim(here, here.shape[0] - 1, here.shape[0], axis=0)

    def add_pair(earlier_total, later_total):
        return earlier_total + later_total

    below = entering(total, "rows", add_pair, jnp.zeros_like(total))
    potential = (here + below) / (field_values.shape[0] * lax.axis_size("rows"))
    return (potential, field_values)


def solution(mesh):
    in_specs = (
        P(("trial", "rows"), "cols", "slabs", None),
        P(("trial", "rows"), "cols", "slabs", None),
    )
    out_specs = (
        P(("trial", "rows"), "cols", "slabs", None),
        P(("trial", "rows"), "cols", "slabs", None),
    )
    return jax.shard_map(
        on_device, mesh=mesh, in_specs=in_specs, out_specs=out_specs, check_vma=False
    )
```

profile of v0, /device:TPU:59, one launch (start us, length us, event | category | flops | bytes accessed | tf_op | source)
XLA Modules:
  0.0 234.4 jit_solution(14719574178035145743)
XLA Ops:
  7.2 0.0 all-gather.3.cloned.1.call-start
  7.2 0.0 copy-start.1
  7.2 1.4 fusion.41
  8.6 1.4 collective-permute-start
  10.1 1.1 fusion.40
  11.2 3.8 %collective-permute-start.2 = (f32[8,1,64,128]{3,2,1,0:T(8,128)S(1)}, f32[8,1,64,128]{3,2,1,0:T(8,128)S(1)}, u32[]{:S(2)}, u32[]{:S(2)}) collective-permute-start(f32[8,1,64,128]{3,2,1,0:T(8,128)S(1)} %get-tuple-element.56), channel_id=1, source_target_pairs={{0,4},{4,8},{8,12},{1,5},{5,9},{9,13},{2,6},{6,10},{10,14},{3,7},{... | collective-permute-start | bytes 786440 | tf_op jit(solution)/shard_map/ppermute | solution.py:17
  14.9 1.3 collective-permute-start.3
  16.2 3.5 %collective-permute-start.1 = (f32[1,16,64,128]{3,2,1,0:T(8,128)S(1)}, f32[1,16,64,128]{3,2,1,0:T(8,128)S(1)}, u32[]{:S(2)}, u32[]{:S(2)}) collective-permute-start(f32[1,16,64,128]{3,2,1,0:T(8,128)S(1)} %get-tuple-element.58), channel_id=1, source_target_pairs={{16,0},{32,16},{48,32},{64,48},{80,64},{96,80},{112,96},{128,112},... | collective-permute-start | bytes 1572872 | tf_op jit(solution)/shard_map/ppermute | solution.py:18
  19.8 1.3 fusion.39
  21.1 7.9 %collective-permute-start.4 = (f32[8,16,1,128]{3,2,1,0:T(1,128)S(1)}, f32[8,16,1,128]{3,2,1,0:T(1,128)S(1)}, u32[]{:S(2)}, u32[]{:S(2)}) collective-permute-start(f32[8,16,1,128]{3,2,1,0:T(1,128)S(1)} %get-tuple-element.54), channel_id=1, source_target_pairs={{0,2},{1,3},{4,6},{5,7},{8,10},{9,11},{12,14},{13,15},{16,18},{17,... | collective-permute-start | bytes 196616 | tf_op jit(solution)/shard_map/ppermute | solution.py:17
  29.0 1.3 collective-permute-start.5
  30.4 0.0 copy-start
  30.5 0.6 constant_dynamic-update-slice_fusion.1
  31.1 3.0 %collective-permute-done.4 = f32[8,16,1,128]{3,2,1,0:T(1,128)S(1)} collective-permute-done((f32[8,16,1,128]{3,2,1,0:T(1,128)S(1)}, f32[8,16,1,128]{3,2,1,0:T(1,128)S(1)}, u32[]{:S(2)}, u32[]{:S(2)}) %collective-permute-start.4) | collective-permute-done | bytes 65568 | tf_op jit(solution)/shard_map/ppermute | solution.py:17
  34.1 5.0 %collective-permute-done.5 = f32[8,16,1,128]{3,2,1,0:T(1,128)S(1)} collective-permute-done((f32[8,16,1,128]{3,2,1,0:T(1,128)S(1)}, f32[8,16,1,128]{3,2,1,0:T(1,128)S(1)}, u32[]{:S(2)}, u32[]{:S(2)}) %collective-permute-start.5) | collective-permute-done | bytes 65568 | tf_op jit(solution)/shard_map/ppermute | solution.py:18
  39.2 12.1 %fusion.27 = f32[8,16,64,128]{3,2,1,0:T(8,128)S(1)} fusion(f32[8,16,64,128]{3,2,1,0:T(8,128)S(1)} %copy-done.1, f32[8,16,1,128]{3,2,1,0:T(1,128)S(1)} %collective-permute-done.5, f32[10,1,64,128]{3,2,1,0:T(8,128)S(1)} %pad.39, f32[10,16,64,128]{3,2,1,0:T(8,128)} %copy-done.4, f32[10,1,64,128]{3,2,1,0:T(8,128)S(1)} %pad.38, ...), kind=kLoop, calls=%fused_computation.65 | loop fusion | flops 31457280 | bytes 19660800 | tf_op jit(solution)/shard_map/add | solution.py:57
  51.3 0.1 fusion.37
  51.4 1.3 collective-permute-start.6
  52.7 4.8 %collective-permute-start.7 = (f32[1,16,64,128]{3,2,1,0:T(8,128)S(1)}, f32[1,16,64,128]{3,2,1,0:T(8,128)S(1)}, u32[]{:S(2)}, u32[]{:S(2)}) collective-permute-start(f32[1,16,64,128]{3,2,1,0:T(8,128)S(1)} %get-tuple-element.51), channel_id=1, source_target_pairs={{16,0},{32,16},{48,32},{64,48},{80,64},{96,80},{112,96},{128,112},... | collective-permute-start | bytes 1572872 | tf_op jit(solution)/shard_map/ppermute | solution.py:18
  57.5 4.9 %collective-permute-start.8 = (f32[8,1,64,128]{3,2,1,0:T(8,128)S(1)}, f32[8,1,64,128]{3,2,1,0:T(8,128)S(1)}, u32[]{:S(2)}, u32[]{:S(2)}) collective-permute-start(f32[8,1,64,128]{3,2,1,0:T(8,128)S(1)} %get-tuple-element.52), channel_id=1, source_target_pairs={{0,4},{4,8},{8,12},{1,5},{5,9},{9,13},{2,6},{6,10},{10,14},{3,7},{... | collective-permute-start | bytes 786440 | tf_op jit(solution)/shard_map/ppermute | solution.py:17
  62.4 1.3 collective-permute-start.9
  63.7 0.1 fusion.36
  63.8 3.2 %collective-permute-start.10 = (f32[8,16,1,128]{3,2,1,0:T(1,128)S(1)}, f32[8,16,1,128]{3,2,1,0:T(1,128)S(1)}, u32[]{:S(2)}, u32[]{:S(2)}) collective-permute-start(f32[8,16,1,128]{3,2,1,0:T(1,128)S(1)} %get-tuple-element.48), channel_id=1, source_target_pairs={{0,2},{1,3},{4,6},{5,7},{8,10},{9,11},{12,14},{13,15},{16,18},{17,... | collective-permute-start | bytes 196616 | tf_op jit(solution)/shard_map/ppermute | solution.py:17
  67.0 1.5 collective-permute-done.8
  68.5 1.3 collective-permute-start.11
  69.8 3.0 %collective-permute-done.9 = f32[8,1,64,128]{3,2,1,0:T(8,128)S(1)} collective-permute-done((f32[8,1,64,128]{3,2,1,0:T(8,128)S(1)}, f32[8,1,64,128]{3,2,1,0:T(8,128)S(1)}, u32[]{:S(2)}, u32[]{:S(2)}) %collective-permute-start.9) | collective-permute-done | bytes 262176 | tf_op jit(solution)/shard_map/ppermute | solution.py:18
  72.8 4.7 %collective-permute-done.11 = f32[8,16,1,128]{3,2,1,0:T(1,128)S(1)} collective-permute-done((f32[8,16,1,128]{3,2,1,0:T(1,128)S(1)}, f32[8,16,1,128]{3,2,1,0:T(1,128)S(1)}, u32[]{:S(2)}, u32[]{:S(2)}) %collective-permute-start.11) | collective-permute-done | bytes 65568 | tf_op jit(solution)/shard_map/ppermute | solution.py:18
  77.6 8.2 %fusion.16 = f32[8,16,64,128]{3,2,1,0:T(8,128)S(1)} fusion(f32[8,16,64,128]{3,2,1,0:T(8,128)S(1)} %fusion.27, f32[8,16,1,128]{3,2,1,0:T(1,128)S(1)} %collective-permute-done.11, f32[10,1,64,128]{3,2,1,0:T(8,128)S(1)} %pad.43, f32[10,1,64,128]{3,2,1,0:T(8,128)S(1)} %pad.42, f32[1,16,64,128]{3,2,1,0:T(8,128)S(1)} %collective-permute-done.7, ...), kind=kLoop, calls=%fused_computation.36 | loop fusion | flops 39845888 | bytes 14417920 | tf_op jit(solution)/shard_map/add | solution.py:57
  85.7 0.1 fusion.34
  85.8 1.3 collective-permute-start.12
  87.1 10.7 %collective-permute-start.13 = (f32[1,16,64,128]{3,2,1,0:T(8,128)S(1)}, f32[1,16,64,128]{3,2,1,0:T(8,128)S(1)}, u32[]{:S(2)}, u32[]{:S(2)}) collective-permute-start(f32[1,16,64,128]{3,2,1,0:T(8,128)S(1)} %get-tuple-element.45), channel_id=1, source_target_pairs={{16,0},{32,16},{48,32},{64,48},{80,64},{96,80},{112,96},{128,112},... | collective-permute-start | bytes 1572872 | tf_op jit(solution)/shard_map/ppermute | solution.py:18
  97.9 6.1 %collective-permute-start.14 = (f32[8,1,64,128]{3,2,1,0:T(8,128)S(1)}, f32[8,1,64,128]{3,2,1,0:T(8,128)S(1)}, u32[]{:S(2)}, u32[]{:S(2)}) collective-permute-start(f32[8,1,64,128]{3,2,1,0:T(8,128)S(1)} %get-tuple-element.46), channel_id=1, source_target_pairs={{0,4},{4,8},{8,12},{1,5},{5,9},{9,13},{2,6},{6,10},{10,14},{3,7},{... | collective-permute-start | bytes 786440 | tf_op jit(solution)/shard_map/ppermute | solution.py:17
  104.0 1.3 collective-permute-start.15
  105.3 0.1 fusion.33
  105.4 1.3 collective-permute-start.16
  106.7 3.4 %collective-permute-done.14 = f32[8,1,64,128]{3,2,1,0:T(8,128)S(1)} collective-permute-done((f32[8,1,64,128]{3,2,1,0:T(8,128)S(1)}, f32[8,1,64,128]{3,2,1,0:T(8,128)S(1)}, u32[]{:S(2)}, u32[]{:S(2)}) %collective-permute-start.14) | collective-permute-done | bytes 262176 | tf_op jit(solution)/shard_map/ppermute | solution.py:17
  110.1 1.3 collective-permute-start.17
  111.4 4.7 %collective-permute-done.15 = f32[8,1,64,128]{3,2,1,0:T(8,128)S(1)} collective-permute-done((f32[8,1,64,128]{3,2,1,0:T(8,128)S(1)}, f32[8,1,64,128]{3,2,1,0:T(8,128)S(1)}, u32[]{:S(2)}, u32[]{:S(2)}) %collective-permute-start.15) | collective-permute-done | bytes 262176 | tf_op jit(solution)/shard_map/ppermute | solution.py:18
  116.1 3.0 %collective-permute-done.17 = f32[8,16,1,128]{3,2,1,0:T(1,128)S(1)} collective-permute-done((f32[8,16,1,128]{3,2,1,0:T(1,128)S(1)}, f32[8,16,1,128]{3,2,1,0:T(1,128)S(1)}, u32[]{:S(2)}, u32[]{:S(2)}) %collective-permute-start.17) | collective-permute-done | bytes 65568 | tf_op jit(solution)/shard_map/ppermute | solution.py:18
  119.1 8.1 %fusion.5 = f32[8,16,64,128]{3,2,1,0:T(8,128)S(1)} fusion(f32[8,16,64,128]{3,2,1,0:T(8,128)S(1)} %fusion.16, f32[8,16,1,128]{3,2,1,0:T(1,128)S(1)} %collective-permute-done.17, f32[10,1,64,128]{3,2,1,0:T(8,128)S(1)} %pad.47, f32[10,1,64,128]{3,2,1,0:T(8,128)S(1)} %pad.46, f32[1,16,64,128]{3,2,1,0:T(8,128)S(1)} %collective-permute-done.13, ...), kind=kLoop, calls=%fused_computation.7 | loop fusion | flops 39845888 | bytes 14417920 | tf_op jit(solution)/shard_map/add | solution.py:57
  127.2 0.0 copy-start.3
  127.3 5.4 %fusion.42 = f32[8,16,64,128]{3,2,1,0:T(8,128)S(1)} fusion(f32[8,16,64,128]{3,2,1,0:T(8,128)S(1)} %fusion.5), kind=kOutput, calls=%fused_computation.95 | output fusion | flops 7340032 | bytes 8388608 | tf_op jit(solution)/shard_map/jit(cumsum)/reduce_window_sum | solution.py:64
  132.7 0.0 copy-start.2
  132.7 2.0 copy-done.2
  134.7 0.9 slice.277
  135.6 0.0 all-gather.3.cloned.1.call-update
  135.6 68.8 %all-gather.3.cloned.1.call-done = f32[16,16,64,128]{3,2,1,0:T(8,128)} async-done(((f32[1,16,64,128]{3,2,1,0:T(8,128)}), f32[16,16,64,128]{3,2,1,0:T(8,128)}) %all-gather.3.cloned.1.call-update) | async-done | bytes 8388624 | tf_op jit(solution)/shard_map/all_gather | solution.py:31
  204.5 18.0 %while.10 = (s32[]{:T(128)}, f32[1,16,64,128]{3,2,1,0:T(8,128)S(1)}, s32[]{:T(128)}, f32[16,1,16,64,128]{4,3,2,1,0:T(8,128)}, s32[]{:T(128)}, /*index=5*/s32[]{:T(128)}, s32[]{:T(128)}) while((s32[]{:T(128)}, f32[1,16,64,128]{3,2,1,0:T(8,128)S(1)}, s32[]{:T(128)}, f32[16,1,16,64,128]{4,3,2,1,0:T(8,128)}, s32[]{:T(128)}, /*index=5*/s32[]{:T(128)}, ...), condition=%wide.region_2.3_spmd, body=%wide.region_1.2_spmd.sunk | while | flops 131077 | bytes 1572987 | solution.py:37
  204.5 1.2 bitcast_add_fusion.2
  205.7 1.2 bitcast_add_fusion.2
  206.9 1.2 bitcast_add_fusion.2
  208.1 1.2 bitcast_add_fusion.2
  209.3 1.2 bitcast_add_fusion.2
  210.5 1.2 bitcast_add_fusion.2
  211.7 1.2 bitcast_add_fusion.2
  212.9 1.2 bitcast_add_fusion.2
  214.1 1.2 bitcast_add_fusion.2
  215.3 1.2 bitcast_add_fusion.2
  216.5 1.2 bitcast_add_fusion.2
  217.7 1.2 bitcast_add_fusion.2
  218.9 1.2 bitcast_add_fusion.2
  220.1 1.2 bitcast_add_fusion.2
  221.3 1.2 bitcast_add_fusion.2
  222.5 5.1 %add_multiply_fusion = f32[8,16,64,128]{3,2,1,0:T(8,128)} fusion(f32[8,16,64,128]{3,2,1,0:T(8,128)} %copy-done.2, f32[16,64,128]{2,1,0:T(8,128)S(1)} %bitcast.9), kind=kLoop, calls=%fused_computation.82 | loop fusion | flops 2097152 | bytes 8912896 | tf_op jit(solution)/shard_map/div | solution.py:71
  (26 shorter events, 0.4 us)
Async XLA Ops:
  7.2 197.2 %all-gather.3.cloned.1.call-start = ((), (), s32[]{:S(2)}) async-start(), calls=%async_computation | async-start | bytes 8912896 | tf_op jit(solution)/shard_map/all_gather | solution.py:31
  7.2 23.2 %copy-start.1 = (f32[8,16,64,128]{3,2,1,0:T(8,128)S(1)}, f32[8,16,64,128]{3,2,1,0:T(8,128)}, u32[]{:S(2)}) copy-start(f32[8,16,64,128]{3,2,1,0:T(8,128)} %param.4) | copy-start | bytes 12582916
  8.6 21.7 %collective-permute-start = (f32[1,16,64,128]{3,2,1,0:T(8,128)S(1)}, f32[1,16,64,128]{3,2,1,0:T(8,128)S(1)}, u32[]{:S(2)}, u32[]{:S(2)}) collective-permute-start(f32[1,16,64,128]{3,2,1,0:T(8,128)S(1)} %get-tuple-element.59), channel_id=1, source_target_pairs={{0,16},{16,32},{32,48},{48,64},{64,80},{80,96},{96,112},{112,128},... | collective-permute-start | bytes 1572872 | tf_op jit(solution)/shard_map/ppermute | solution.py:17
  11.2 17.8 %collective-permute-start.2 = (f32[8,1,64,128]{3,2,1,0:T(8,128)S(1)}, f32[8,1,64,128]{3,2,1,0:T(8,128)S(1)}, u32[]{:S(2)}, u32[]{:S(2)}) collective-permute-start(f32[8,1,64,128]{3,2,1,0:T(8,128)S(1)} %get-tuple-element.56), channel_id=1, source_target_pairs={{0,4},{4,8},{8,12},{1,5},{5,9},{9,13},{2,6},{6,10},{10,14},{3,7},{... | collective-permute-start | bytes 786440 | tf_op jit(solution)/shard_map/ppermute | solution.py:17
  14.9 15.4 %collective-permute-start.3 = (f32[8,1,64,128]{3,2,1,0:T(8,128)S(1)}, f32[8,1,64,128]{3,2,1,0:T(8,128)S(1)}, u32[]{:S(2)}, u32[]{:S(2)}) collective-permute-start(f32[8,1,64,128]{3,2,1,0:T(8,128)S(1)} %get-tuple-element.57), channel_id=1, source_target_pairs={{4,0},{8,4},{12,8},{5,1},{9,5},{13,9},{6,2},{10,6},{14,10},{7,3},{... | collective-permute-start | bytes 786440 | tf_op jit(solution)/shard_map/ppermute | solution.py:18
  16.2 14.8 %collective-permute-start.1 = (f32[1,16,64,128]{3,2,1,0:T(8,128)S(1)}, f32[1,16,64,128]{3,2,1,0:T(8,128)S(1)}, u32[]{:S(2)}, u32[]{:S(2)}) collective-permute-start(f32[1,16,64,128]{3,2,1,0:T(8,128)S(1)} %get-tuple-element.58), channel_id=1, source_target_pairs={{16,0},{32,16},{48,32},{64,48},{80,64},{96,80},{112,96},{128,112},... | collective-permute-start | bytes 1572872 | tf_op jit(solution)/shard_map/ppermute | solution.py:18
  21.1 13.1 %collective-permute-start.4 = (f32[8,16,1,128]{3,2,1,0:T(1,128)S(1)}, f32[8,16,1,128]{3,2,1,0:T(1,128)S(1)}, u32[]{:S(2)}, u32[]{:S(2)}) collective-permute-start(f32[8,16,1,128]{3,2,1,0:T(1,128)S(1)} %get-tuple-element.54), channel_id=1, source_target_pairs={{0,2},{1,3},{4,6},{5,7},{8,10},{9,11},{12,14},{13,15},{16,18},{17,... | collective-permute-start | bytes 196616 | tf_op jit(solution)/shard_map/ppermute | solution.py:17
  29.0 10.2 %collective-permute-start.5 = (f32[8,16,1,128]{3,2,1,0:T(1,128)S(1)}, f32[8,16,1,128]{3,2,1,0:T(1,128)S(1)}, u32[]{:S(2)}, u32[]{:S(2)}) collective-permute-start(f32[8,16,1,128]{3,2,1,0:T(1,128)S(1)} %get-tuple-element.55), channel_id=1, source_target_pairs={{2,0},{3,1},{6,4},{7,5},{10,8},{11,9},{14,12},{15,13},{18,16},{19,... | collective-permute-start | bytes 196616 | tf_op jit(solution)/shard_map/ppermute | solution.py:18
  30.4 8.7 %copy-start = (f32[8,16,64,128]{3,2,1,0:T(8,128)S(1)}, f32[8,16,64,128]{3,2,1,0:T(8,128)}, u32[]{:S(2)}) copy-start(f32[8,16,64,128]{3,2,1,0:T(8,128)} %param.5) | copy-start | bytes 12582916
  31.1 3.0 %copy-start.4 = (f32[10,16,64,128]{3,2,1,0:T(8,128)}, f32[10,16,64,128]{3,2,1,0:T(8,128)S(1)}, u32[]{:S(2)}) copy-start(f32[10,16,64,128]{3,2,1,0:T(8,128)S(1)} %constant_dynamic-update-slice_fusion) | copy-start | bytes 15728644
  51.4 26.2 %collective-permute-start.6 = (f32[1,16,64,128]{3,2,1,0:T(8,128)S(1)}, f32[1,16,64,128]{3,2,1,0:T(8,128)S(1)}, u32[]{:S(2)}, u32[]{:S(2)}) collective-permute-start(f32[1,16,64,128]{3,2,1,0:T(8,128)S(1)} %get-tuple-element.50), channel_id=1, source_target_pairs={{0,16},{16,32},{32,48},{48,64},{64,80},{80,96},{96,112},{112,128},... | collective-permute-start | bytes 1572872 | tf_op jit(solution)/shard_map/ppermute | solution.py:17
  52.7 24.9 %collective-permute-start.7 = (f32[1,16,64,128]{3,2,1,0:T(8,128)S(1)}, f32[1,16,64,128]{3,2,1,0:T(8,128)S(1)}, u32[]{:S(2)}, u32[]{:S(2)}) collective-permute-start(f32[1,16,64,128]{3,2,1,0:T(8,128)S(1)} %get-tuple-element.51), channel_id=1, source_target_pairs={{16,0},{32,16},{48,32},{64,48},{80,64},{96,80},{112,96},{128,112},... | collective-permute-start | bytes 1572872 | tf_op jit(solution)/shard_map/ppermute | solution.py:18
  57.5 11.0 %collective-permute-start.8 = (f32[8,1,64,128]{3,2,1,0:T(8,128)S(1)}, f32[8,1,64,128]{3,2,1,0:T(8,128)S(1)}, u32[]{:S(2)}, u32[]{:S(2)}) collective-permute-start(f32[8,1,64,128]{3,2,1,0:T(8,128)S(1)} %get-tuple-element.52), channel_id=1, source_target_pairs={{0,4},{4,8},{8,12},{1,5},{5,9},{9,13},{2,6},{6,10},{10,14},{3,7},{... | collective-permute-start | bytes 786440 | tf_op jit(solution)/shard_map/ppermute | solution.py:17
  62.4 10.4 %collective-permute-start.9 = (f32[8,1,64,128]{3,2,1,0:T(8,128)S(1)}, f32[8,1,64,128]{3,2,1,0:T(8,128)S(1)}, u32[]{:S(2)}, u32[]{:S(2)}) collective-permute-start(f32[8,1,64,128]{3,2,1,0:T(8,128)S(1)} %get-tuple-element.53), channel_id=1, source_target_pairs={{4,0},{8,4},{12,8},{5,1},{9,5},{13,9},{6,2},{10,6},{14,10},{7,3},{... | collective-permute-start | bytes 786440 | tf_op jit(solution)/shard_map/ppermute | solution.py:18
  63.8 9.0 %collective-permute-start.10 = (f32[8,16,1,128]{3,2,1,0:T(1,128)S(1)}, f32[8,16,1,128]{3,2,1,0:T(1,128)S(1)}, u32[]{:S(2)}, u32[]{:S(2)}) collective-permute-start(f32[8,16,1,128]{3,2,1,0:T(1,128)S(1)} %get-tuple-element.48), channel_id=1, source_target_pairs={{0,2},{1,3},{4,6},{5,7},{8,10},{9,11},{12,14},{13,15},{16,18},{17,... | collective-permute-start | bytes 196616 | tf_op jit(solution)/shard_map/ppermute | solution.py:17
  68.5 9.1 %collective-permute-start.11 = (f32[8,16,1,128]{3,2,1,0:T(1,128)S(1)}, f32[8,16,1,128]{3,2,1,0:T(1,128)S(1)}, u32[]{:S(2)}, u32[]{:S(2)}) collective-permute-start(f32[8,16,1,128]{3,2,1,0:T(1,128)S(1)} %get-tuple-element.49), channel_id=1, source_target_pairs={{2,0},{3,1},{6,4},{7,5},{10,8},{11,9},{14,12},{15,13},{18,16},{19,... | collective-permute-start | bytes 196616 | tf_op jit(solution)/shard_map/ppermute | solution.py:18
  85.8 33.3 %collective-permute-start.12 = (f32[1,16,64,128]{3,2,1,0:T(8,128)S(1)}, f32[1,16,64,128]{3,2,1,0:T(8,128)S(1)}, u32[]{:S(2)}, u32[]{:S(2)}) collective-permute-start(f32[1,16,64,128]{3,2,1,0:T(8,128)S(1)} %get-tuple-element.44), channel_id=1, source_target_pairs={{0,16},{16,32},{32,48},{48,64},{64,80},{80,96},{96,112},{112,128},... | collective-permute-start | bytes 1572872 | tf_op jit(solution)/shard_map/ppermute | solution.py:17
  87.1 32.0 %collective-permute-start.13 = (f32[1,16,64,128]{3,2,1,0:T(8,128)S(1)}, f32[1,16,64,128]{3,2,1,0:T(8,128)S(1)}, u32[]{:S(2)}, u32[]{:S(2)}) collective-permute-start(f32[1,16,64,128]{3,2,1,0:T(8,128)S(1)} %get-tuple-element.45), channel_id=1, source_target_pairs={{16,0},{32,16},{48,32},{64,48},{80,64},{96,80},{112,96},{128,112},... | collective-permute-start | bytes 1572872 | tf_op jit(solution)/shard_map/ppermute | solution.py:18
  97.9 12.2 %collective-permute-start.14 = (f32[8,1,64,128]{3,2,1,0:T(8,128)S(1)}, f32[8,1,64,128]{3,2,1,0:T(8,128)S(1)}, u32[]{:S(2)}, u32[]{:S(2)}) collective-permute-start(f32[8,1,64,128]{3,2,1,0:T(8,128)S(1)} %get-tuple-element.46), channel_id=1, source_target_pairs={{0,4},{4,8},{8,12},{1,5},{5,9},{9,13},{2,6},{6,10},{10,14},{3,7},{... | collective-permute-start | bytes 786440 | tf_op jit(solution)/shard_map/ppermute | solution.py:17
  104.0 12.1 %collective-permute-start.15 = (f32[8,1,64,128]{3,2,1,0:T(8,128)S(1)}, f32[8,1,64,128]{3,2,1,0:T(8,128)S(1)}, u32[]{:S(2)}, u32[]{:S(2)}) collective-permute-start(f32[8,1,64,128]{3,2,1,0:T(8,128)S(1)} %get-tuple-element.47), channel_id=1, source_target_pairs={{4,0},{8,4},{12,8},{5,1},{9,5},{13,9},{6,2},{10,6},{14,10},{7,3},{... | collective-permute-start | bytes 786440 | tf_op jit(solution)/shard_map/ppermute | solution.py:18
  105.4 10.7 %collective-permute-start.16 = (f32[8,16,1,128]{3,2,1,0:T(1,128)S(1)}, f32[8,16,1,128]{3,2,1,0:T(1,128)S(1)}, u32[]{:S(2)}, u32[]{:S(2)}) collective-permute-start(f32[8,16,1,128]{3,2,1,0:T(1,128)S(1)} %get-tuple-element.42), channel_id=1, source_target_pairs={{0,2},{1,3},{4,6},{5,7},{8,10},{9,11},{12,14},{13,15},{16,18},{17,... | collective-permute-start | bytes 196616 | tf_op jit(solution)/shard_map/ppermute | solution.py:17
  110.1 9.0 %collective-permute-start.17 = (f32[8,16,1,128]{3,2,1,0:T(1,128)S(1)}, f32[8,16,1,128]{3,2,1,0:T(1,128)S(1)}, u32[]{:S(2)}, u32[]{:S(2)}) collective-permute-start(f32[8,16,1,128]{3,2,1,0:T(1,128)S(1)} %get-tuple-element.43), channel_id=1, source_target_pairs={{2,0},{3,1},{6,4},{7,5},{10,8},{11,9},{14,12},{15,13},{18,16},{19,... | collective-permute-start | bytes 196616 | tf_op jit(solution)/shard_map/ppermute | solution.py:18
  127.2 5.4 %copy-start.3 = (f32[8,16,64,128]{3,2,1,0:T(8,128)}, f32[8,16,64,128]{3,2,1,0:T(8,128)S(1)}, u32[]{:S(2)}) copy-start(f32[8,16,64,128]{3,2,1,0:T(8,128)S(1)} %fusion.5) | copy-start | bytes 12582916
  132.7 2.0 copy-start.2
Sparse Core Ops, SparseCore 0:
  135.7 68.6 all-gather.2
where the time goes:
time: 236 us; the launch traced here: 234 us
  waiting for transfers between devices  97.1 us (41%)
  starting transfers between devices  58 us (25%)
  other arithmetic  56.6 us (24%)
  between operations  14.5 us (6%)
  local copies, waits for them, and re-layouts  7.99 us (3%)
    all_gather x1, waiting for transfers between devices, entering(): gathered = lax.all_gather(part, axis)  68.8 us
    ppermute x9, starting transfers between devices, with_halo(): lax.ppermute(last, axis, up)  31.2 us
    add x3, other arithmetic, march_step(): return middle + 0.1 * spread + 0.2 * middle * (1.0 - middle * crowding)  28.4 us
    ppermute x9, starting transfers between devices, with_halo(): lax.ppermute(initial, axis, [(b, a) for a, b in up])  26.7 us
    ppermute x9, waiting for transfers between devices, with_halo(): lax.ppermute(initial, axis, [(b, a) for a, b in up])  20.4 us
    add x15, other arithmetic, add_pair(): return earlier_total + later_total  17.7 us
    ppermute x9, waiting for transfers between devices, with_halo(): lax.ppermute(last, axis, up)  7.91 us
    another operation x1, other arithmetic, on_device(): here = jnp.cumsum(field_values, axis=0)  5.41 us
  transfers between devices with their start and end apart: 19, of which 9 were waited for; matrix products, arithmetic and copies ran while one was open for 1% of the time, Pallas kernels for 0%

commit v1 on v0

v1 whole, which is shorter than its diff:
```python
import functools

import jax
import jax.numpy as jnp
from jax import lax
from jax.experimental import pallas as pl
from jax.experimental.pallas import tpu as pltpu
from jax.sharding import PartitionSpec as P

MESH = pl.DeviceIdType.MESH
F32 = jnp.float32
STEPS = 3
NJ, NI, NK, NL = 8, 16, 64, 128
K0 = 8
EDGE = ((0, 4), (12, 4))
MID = ((4, 8),)
GROUPS = EDGE + MID
CELLS = pl.ds(K0, NK)
N_SEM = 12
UP, DOWN, I_UP, I_DOWN, KF = 0, 3, 6, 7, 8


def rows_of(groups, body):
    for start, count in groups:
        lax.fori_loop(start, start + count, lambda i, _: (body(i), 0)[1], 0)


def exchange_kernel(fv, cr, out, below, u0, u1, u2, c, kf, kh, tot, tot_p, x_in, x_out, p_in, z, z_p, load_sem, s_sem, r_sem, ps_sem, pr_sem):
    r, col, slab = lax.axis_index("rows"), lax.axis_index("cols"), lax.axis_index("slabs")
    core = lax.rem(r, 2)
    x_lo = lax.rem(lax.div(r, 2), 2)
    y = lax.div(r, 4)
    u = (u0, u1, u2)
    other_core = {"rows": r + 1 - 2 * core}
    other_chip = {"rows": r + 2 - 4 * x_lo}

    has = {UP: r < 15, DOWN: r > 0, I_UP: col < 3, I_DOWN: col > 0}
    to = {UP: {"rows": r + 1}, DOWN: {"rows": r - 1}, I_UP: {"cols": col + 1}, I_DOWN: {"cols": col - 1}}
    barrier = pltpu.get_barrier_semaphore()
    count = jnp.int32(2)
    for way in (UP, DOWN, I_UP, I_DOWN):
        count = count + jnp.where(has[way], 1, 0)

        @pl.when(has[way])
        def _(way=way):
            pl.semaphore_signal(barrier, 1, device_id=to[way], device_id_type=MESH)

    for ok, dst in ((y < 3, {"rows": r + 4}), (y > 0, {"rows": r - 4})):
        count = count + jnp.where(ok, 1, 0)

        @pl.when(ok)
        def _(dst=dst):
            pl.semaphore_signal(barrier, 1, device_id=dst, device_id_type=MESH)

    pl.semaphore_signal(barrier, 1, device_id={"slabs": 1 - slab}, device_id_type=MESH)
    pl.semaphore_signal(barrier, 1, device_id=other_chip, device_id_type=MESH)

    load_u = pltpu.make_async_copy(fv, u0.at[pl.ds(1, NJ), pl.ds(1, NI), CELLS], load_sem.at[0])
    load_c = pltpu.make_async_copy(cr, c, load_sem.at[1])
    load_u.start()
    load_c.start()

    edge_row = jnp.where(slab == 0, K0 - 1, K0 + NK)
    halo_row = jnp.where(slab == 0, K0 + NK, K0 - 1)
    face_row = jnp.where(slab == 0, K0 + NK - 1, K0)
    zero_plane = jnp.zeros((NK, NL), F32)
    zero_line = jnp.zeros((1, NL), F32)

    def zero_lines(i):
        for b in u:
            for j in range(NJ):
                b[j + 1, i + 1, pl.ds(edge_row, 1), :] = zero_line

    rows_of(((0, NI),), zero_lines)

    def zero_j(plane):
        def body(i):
            for b in u:
                b[plane, i + 1, CELLS, :] = zero_plane

        rows_of(((0, NI),), body)

    def zero_i(row):
        def body(j):
            for b in u:
                b[j + 1, row, CELLS, :] = zero_plane

        rows_of(((0, NJ),), body)

    pl.when(r == 0)(lambda: zero_j(0))
    pl.when(r == 15)(lambda: zero_j(NJ + 1))
    pl.when(col == 0)(lambda: zero_i(0))
    pl.when(col == 3)(lambda: zero_i(NI + 1))

    def remote(src, dst, s, n, device):
        return pltpu.make_async_remote_copy(src, dst, s_sem.at[s, n], r_sem.at[s, n], device_id=device, device_id_type=MESH)

    def j_copy(s, way, g):
        start, n = GROUPS[g]
        rows = pl.ds(start + 1, n)
        a, b = (NJ, 0) if way == UP else (1, NJ + 1)
        return remote(u[s].at[a, rows, CELLS], u[s].at[b, rows, CELLS], s, way + g, to[way])

    def i_copy(s, way):
        a, b = (NI, 0) if way == I_UP else (1, NI + 1)
        return remote(u[s].at[pl.ds(1, NJ), a, CELLS], u[s].at[pl.ds(1, NJ), b, CELLS], s, way, to[way])

    def k_copy(s, g):
        start, n = GROUPS[g]
        rows = pl.ds(start, n)
        return remote(kf.at[s, rows], kh.at[s, rows], s, KF + g, {"slabs": 1 - slab})

    def take_k(s, groups):
        def body(i):
            for j in range(NJ):
                kf[s, i, pl.ds(j, 1), :] = u[s][j + 1, i + 1, pl.ds(face_row, 1), :]

        rows_of(groups, body)

    def put_k(s, groups):
        def body(i):
            for j in range(NJ):
                u[s][j + 1, i + 1, pl.ds(halo_row, 1), :] = kh[s, i, pl.ds(j, 1), :]

        rows_of(groups, body)

    def each_j(s, gs, act):
        for g in gs:
            for way in (UP, DOWN):

                @pl.when(has[way])
                def _(way=way, g=g):
                    act(j_copy(s, way, g))

    def send_i(s):
        for way in (I_UP, I_DOWN):

            @pl.when(has[way])
            def _(way=way):
                i_copy(s, way).start()

    def send_k(s, gs):
        for g in gs:
            k_copy(s, g).start()

    def recv_i(s):
        for way, back in ((I_UP, I_DOWN), (I_DOWN, I_UP)):

            @pl.when(has[back])
            def _(way=way):
                i_copy(s, way).wait_recv()

    def recv_j(s, gs):
        for g in gs:
            for way, back in ((UP, DOWN), (DOWN, UP)):

                @pl.when(has[back])
                def _(way=way, g=g):
                    j_copy(s, way, g).wait_recv()

    def recv_k(s, gs):
        for g in gs:
            k_copy(s, g).wait_recv()

    def march(s, groups):
        b = u[s]

        def body(i):
            for k in range(0, NK, 8):
                here, lower, upper = pl.ds(K0 + k, 8), pl.ds(K0 + k - 1, 8), pl.ds(K0 + k + 1, 8)
                prev, mid = b[0, i + 1, here, :], b[1, i + 1, here, :]
                for j in range(1, NJ + 1):
                    following = b[j + 1, i + 1, here, :]
                    near = (prev + following) + (b[j, i, here, :] + b[j, i + 2, here, :])
                    near = near + (b[j, i + 1, lower, :] + b[j, i + 1, upper, :])
                    new = mid * (0.6 - 0.2 * (mid * c[j - 1, i, pl.ds(k, 8), :])) + 0.1 * near
                    if s + 1 < STEPS:
                        u[s + 1][j, i + 1, here, :] = new
                    else:
                        out[j - 1, i, pl.ds(k, 8), :] = new
                    prev, mid = mid, following

        rows_of(groups, body)

    first = jnp.where(r == 0, 0.1, 0.0).astype(F32)
    later = jnp.where(r == 0, 0.0, 0.1).astype(F32)

    def block_totals(groups):
        b = u[2]

        def body(i):
            for k in range(0, NK, 8):
                here, lower, upper = pl.ds(K0 + k, 8), pl.ds(K0 + k - 1, 8), pl.ds(K0 + k + 1, 8)
                own, near = None, None
                for j in range(1, NJ + 1):
                    mid = b[j, i + 1, here, :]
                    term = mid * (0.8 - 0.2 * (mid * c[j - 1, i, pl.ds(k, 8), :]))
                    if j == 1:
                        term = term - first * mid
                    beside = (b[j, i, here, :] + b[j, i + 2, here, :]) + (b[j, i + 1, lower, :] + b[j, i + 1, upper, :])
                    own = term if own is None else own + term
                    near = beside if near is None else near + beside
                tot[i, pl.ds(k, 8), :] = own + 0.1 * near

        rows_of(groups, body)

    def p_copy(n, src, dst, device):
        return pltpu.make_async_remote_copy(src, dst, ps_sem.at[n], pr_sem.at[n], device_id=device, device_id_type=MESH)

    parts = ((4 + 4 * core, 4), (1 + 11 * core, 3), (15 * core, 1))
    parts_p = ((8 - 4 * core, 4), (12 - 11 * core, 3), (15 - 15 * core, 1))

    def t_copy(n):
        rows = (pl.ds(1, 14), pl.ds(0, 1), pl.ds(15, 1))[n]
        return p_copy(n, tot.at[rows], tot_p.at[rows], other_core)

    def y_copy(n):
        rows = pl.ds(*parts[n])
        return p_copy(3 + n, x_out.at[rows], x_in.at[rows], {"rows": r + 4})

    def x_copy(n, src):
        rows = pl.ds(*parts[n])
        return p_copy(6 + n, src.at[rows], p_in.at[rows], other_chip)

    def z_copy(n, mine=True):
        rows = pl.ds(*(parts if mine else parts_p)[n])
        return p_copy(9 + n, z.at[rows], z_p.at[rows], other_core)

    sends_x = ((x_lo == 0), (x_lo == 1) & (y > 0))
    takes_x = (x_lo == 1) | (y > 0)

    def chain(n):
        start, rows = parts[n]
        own = ((start, rows),)

        @pl.when(y > 0)
        def _():
            y_copy(n).wait_recv()

            def body(i):
                x_out[i] = x_in[i] + (tot[i] + tot_p[i])

            rows_of(own, body)

        @pl.when(y == 0)
        def _():
            def body(i):
                x_out[i] = tot[i] + tot_p[i]

            rows_of(own, body)

        pl.when(y < 3)(lambda: y_copy(n).start())
        pl.when(sends_x[0])(lambda: x_copy(n, x_out).start())
        pl.when(sends_x[1])(lambda: x_copy(n, x_in).start())

    def combine(n):
        own = (parts[n],)

        @pl.when(takes_x)
        def _():
            x_copy(n, x_out).wait_recv()

        @pl.when(y > 0)
        def _():
            def body(i):
                z[i] = x_in[i] + p_in[i]

            rows_of(own, body)

        @pl.when((y == 0) & (x_lo == 1))
        def _():
            def body(i):
                z[i] = p_in[i]

            rows_of(own, body)

        @pl.when((y == 0) & (x_lo == 0))
        def _():
            def body(i):
                z[i] = zero_plane

            rows_of(own, body)

        z_copy(n).start()

    pl.semaphore_wait(barrier, count)
    load_u.wait()
    send_i(0)
    take_k(0, ((0, NI),))
    send_k(0, (0, 1, 2))
    each_j(0, (0, 1, 2), lambda copy: copy.start())
    load_c.wait()

    for s in range(STEPS):
        if s == 2:
            recv_k(2, (0, 1, 2))
            put_k(2, ((0, NI),))
            block_totals(((1, 14),))
            t_copy(0).start()
            t_copy(0).wait_recv()
            chain(0)
            chain(1)
            recv_i(2)
            block_totals(((0, 1), (15, 1)))
            t_copy(1).start()
            t_copy(2).start()
            t_copy(1).wait_recv()
            t_copy(2).wait_recv()
            chain(2)
        else:
            recv_k(s, (0, 1))
            put_k(s, EDGE)
            recv_i(s)
        recv_j(s, (0, 1))
        march(s, EDGE)
        if s < 2:
            send_i(s + 1)
            take_k(s + 1, EDGE)
            send_k(s + 1, (0, 1))
            each_j(s + 1, (0, 1), lambda copy: copy.start())
            recv_k(s, (2,))
            put_k(s, MID)
        recv_j(s, (2,))
        march(s, MID)
        if s < 2:
            take_k(s + 1, MID)
            send_k(s + 1, (2,))
            each_j(s + 1, (2,), lambda copy: copy.start())

    for n in range(3):
        combine(n)

    def finish(groups, get):
        def body(i):
            below[i] = get(i) + later * (u2[1, i + 1, CELLS, :] - u2[0, i + 1, CELLS, :])

        rows_of(groups, body)

    def finish_part(part, src):
        pl.when(core == 0)(lambda: finish((part,), lambda i: src[i]))
        pl.when(core == 1)(lambda: finish((part,), lambda i: src[i] + tot_p[i]))

    for n in range(3):
        finish_part(parts[n], z)
    for n in range(3):
        z_copy(n, mine=False).wait_recv()
        finish_part(parts_p[n], z_p)

    for s in range(STEPS):
        each_j(s, (0, 1, 2), lambda copy: copy.wait_send())
        for way in (I_UP, I_DOWN):

            @pl.when(has[way])
            def _(way=way, s=s):
                i_copy(s, way).wait_send()

        for g in range(3):
            k_copy(s, g).wait_send()
    for n in range(3):
        t_copy(n).wait_send()
        z_copy(n).wait_send()
        pl.when(y < 3)(lambda n=n: y_copy(n).wait_send())
        pl.when(sends_x[0] | sends_x[1])(lambda n=n: x_copy(n, x_out).wait_send())


def write_kernel(v, below, pot, end, pot_v, sem):
    copies = [pltpu.make_async_copy(v, end, sem.at[0])]
    copies[0].start()
    for q in range(4):

        def body(i, _):
            for k in range(0, NK, 8):
                here = pl.ds(k, 8)
                total = below[i, here, :]
                for j in range(NJ):
                    total = total + v[j, i, here, :]
                    pot_v[j, i, here, :] = total * (1.0 / 128.0)
            return 0

        lax.fori_loop(4 * q, 4 * q + 4, body, 0)
        rows = pl.ds(4 * q, 4)
        copy = pltpu.make_async_copy(pot_v.at[:, rows], pot.at[:, rows], sem.at[1 + q])
        copy.start()
        copies.append(copy)
    for copy in copies:
        copy.wait()


def on_device(field_values, crowding):
    block = (NJ, NI, NK, NL)
    plane = (NI, NK, NL)
    padded = (NJ + 2, NI + 2, NK + 16, NL)
    vmem = pl.BlockSpec(memory_space=pltpu.VMEM)
    hbm = pl.BlockSpec(memory_space=pltpu.HBM)
    sems = pltpu.SemaphoreType.DMA
    out, below = pl.pallas_call(
        exchange_kernel,
        out_shape=(pltpu.VMEM(block, F32), pltpu.VMEM(plane, F32)),
        in_specs=[hbm, hbm],
        out_specs=(vmem, vmem),
        scratch_shapes=[pltpu.VMEM(padded, F32)] * 3
        + [pltpu.VMEM(block, F32)]
        + [pltpu.VMEM((STEPS, NI, NJ, NL), F32)] * 2
        + [pltpu.VMEM(plane, F32)] * 7
        + [sems((2,)), sems((STEPS, N_SEM)), sems((STEPS, N_SEM)), sems((12,)), sems((12,))],
        compiler_params=pltpu.CompilerParams(collective_id=1, has_side_effects=True, vmem_limit_bytes=44 * 2**20),
        name="exchange",
    )(field_values, crowding)
    full = jax.ShapeDtypeStruct(block, F32)
    return pl.pallas_call(
        write_kernel,
        out_shape=(full, full),
        in_specs=[vmem, vmem],
        out_specs=(hbm, hbm),
        scratch_shapes=[pltpu.VMEM(block, F32), sems((5,))],
        compiler_params=pltpu.CompilerParams(vmem_limit_bytes=16 * 2**20),
        name="write",
    )(out, below)


def solution(mesh):
    spec = P(("trial", "rows"), "cols", "slabs", None)
    return jax.shard_map(on_device, mesh=mesh, in_specs=(spec, spec), out_specs=(spec, spec), check_vma=False)
```

time: 236 us -> 95.3 us (0.40)
  waiting for transfers between devices: 97.1 us -> 0 us
  Pallas kernels: 0 us -> 92.4 us
  starting transfers between devices: 58 us -> 0 us
  other arithmetic: 56.6 us -> 0 us
  between operations: 14.5 us -> 0.65 us
  local copies, waits for them, and re-layouts: 7.99 us -> 2.18 us
    pallas_call x0 -> x2, Pallas kernels: none -> 92.4 us  [the longest x1 89 us: on_device(): pl.pallas_call(exchange_kernel, out_shape=(pltpu.VMEM(block, F32), pltpu....]
    all_gather x1 -> x0, waiting for transfers between devices: 68.8 us -> none  [entering(): gathered = lax.all_gather(part, axis)]
    ppermute x18 -> x0, starting transfers between devices: 57.9 us -> none  [the longest x9 31.2 us: with_halo(): lax.ppermute(last, axis, up)]
    add x18 -> x0, other arithmetic: 46 us -> none  [the longest x3 28.4 us: march_step(): return middle + 0.1 * spread + 0.2 * middle * (1.0 - middle * crowding)]
    ppermute x18 -> x0, waiting for transfers between devices: 28.3 us -> none  [the longest x9 20.4 us: with_halo(): lax.ppermute(initial, axis, [(b, a) for a, b in up])]
    another operation x1 -> x0, other arithmetic: 5.41 us -> none  [on_device(): here = jnp.cumsum(field_values, axis=0)]
    div x1 -> x0, other arithmetic: 5.13 us -> none  [on_device(): potential = (here + below) / (field_values.shape[0] * lax.axis_size('rows'))]
    slice x10 -> x0, local copies, waits for them, and re-layouts: 5.12 us -> none  [the longest x8 2.82 us: with_halo(): last = lax.slice_in_dim(shard, length - width, length, axis=dim)]
  transfers between devices with their start and end apart: 19 -> 0, of which waited for: 9 -> 0; matrix products, arithmetic and copies ran while one was open for 1% -> 0% of each run, Pallas kernels for 0% -> 0%
where the time goes in v1:
time: 95.3 us; the launch traced here: 95.2 us
  Pallas kernels  92.4 us (97%)
  local copies, waits for them, and re-layouts  2.18 us (2%)
    pallas_call x1, Pallas kernels, on_device(): pl.pallas_call(exchange_kernel, out_shape=(pltpu.VMEM(block, F32), pltpu....  89 us
    pallas_call x1, Pallas kernels, on_device(): pl.pallas_call(write_kernel, out_shape=(full, full), in_specs=[vmem, vmem...  3.34 us
    unnamed x2, local copies, waits for them, and re-layouts  2.18 us

profile of v1, /device:TPU:59, one launch (start us, length us, event | category | flops | bytes accessed | tf_op | source)
XLA Modules:
  0.0 95.2 jit_solution(5992268711170494654)
XLA Ops:
  0.6 0.0 copy-start
  0.6 2.2 %copy-done = f32[8,16,64,128]{3,2,1,0:T(8,128)S(1)} copy-done((f32[8,16,64,128]{3,2,1,0:T(8,128)S(1)}, f32[8,16,64,128]{3,2,1,0:T(8,128)}, u32[]{:S(2)}) %copy-start) | copy-done | bytes 4194328
  2.8 89.0 %exchange.1 = (f32[8,16,64,128]{3,2,1,0:T(8,128)S(1)}, f32[16,64,128]{2,1,0:T(8,128)S(1)}) custom-call(f32[8,16,64,128]{3,2,1,0:T(8,128)S(1)} %copy-done, f32[8,16,64,128]{3,2,1,0:T(8,128)} %cr.1), custom_call_target="tpu_custom_call" | custom-call | tf_op jit(solution)/shard_map/exchange/pallas_call | solution.py:396
  91.8 3.3 %write.1 = (f32[8,16,64,128]{3,2,1,0:T(8,128)}, f32[8,16,64,128]{3,2,1,0:T(8,128)}) custom-call(f32[8,16,64,128]{3,2,1,0:T(8,128)S(1)} %get-tuple-element.4.v, f32[16,64,128]{2,1,0:T(8,128)S(1)} %get-tuple-element.5.below), custom_call_target="tpu_custom_call" | custom-call | tf_op jit(solution)/shard_map/write/pallas_call | solution.py:410
Async XLA Ops:
  0.6 2.2 %copy-start = (f32[8,16,64,128]{3,2,1,0:T(8,128)S(1)}, f32[8,16,64,128]{3,2,1,0:T(8,128)}, u32[]{:S(2)}) copy-start(f32[8,16,64,128]{3,2,1,0:T(8,128)} %fv.1) | copy-start | bytes 12582916

commit v2 on v1

--- a/solution.py
+++ b/solution.py
@@ -16,8 +16,11 @@
 MID = ((4, 8),)
 GROUPS = EDGE + MID
 CELLS = pl.ds(K0, NK)
-N_SEM = 12
-UP, DOWN, I_UP, I_DOWN, KF = 0, 3, 6, 7, 8
+N_SEM = 15
+UP, DOWN, I_UP, I_DOWN, KF, RELAY, FORWARD = 0, 3, 6, 8, 10, 13, 14
+
+
+CHUNKS = 6
 
 
 def rows_of(groups, body):
@@ -25,7 +28,7 @@
         lax.fori_loop(start, start + count, lambda i, _: (body(i), 0)[1], 0)
 
 
-def exchange_kernel(fv, cr, out, below, u0, u1, u2, c, kf, kh, tot, tot_p, x_in, x_out, p_in, z, z_p, load_sem, s_sem, r_sem, ps_sem, pr_sem):
+def exchange_kernel(fv, cr, out, below, u0, u1, u2, c, kf, kh, held, tot, tot_p, x_in, x_out, p_in, z, z_p, load_sem, s_sem, r_sem, ps_sem, pr_sem):
     r, col, slab = lax.axis_index("rows"), lax.axis_index("cols"), lax.axis_index("slabs")
     core = lax.rem(r, 2)
     x_lo = lax.rem(lax.div(r, 2), 2)
@@ -33,11 +36,13 @@
     u = (u0, u1, u2)
     other_core = {"rows": r + 1 - 2 * core}
     other_chip = {"rows": r + 2 - 4 * x_lo}
+    via = {"rows": r + 2 - 4 * x_lo, "cols": col + 1 - 2 * lax.rem(col, 2)}
+    onward = {"rows": r + 2 - 4 * x_lo, "cols": lax.rem(col + 2, 4)}
 
     has = {UP: r < 15, DOWN: r > 0, I_UP: col < 3, I_DOWN: col > 0}
     to = {UP: {"rows": r + 1}, DOWN: {"rows": r - 1}, I_UP: {"cols": col + 1}, I_DOWN: {"cols": col - 1}}
     barrier = pltpu.get_barrier_semaphore()
-    count = jnp.int32(2)
+    count = jnp.int32(4)
     for way in (UP, DOWN, I_UP, I_DOWN):
         count = count + jnp.where(has[way], 1, 0)
 
@@ -53,7 +58,8 @@
             pl.semaphore_signal(barrier, 1, device_id=dst, device_id_type=MESH)
 
     pl.semaphore_signal(barrier, 1, device_id={"slabs": 1 - slab}, device_id_type=MESH)
-    pl.semaphore_signal(barrier, 1, device_id=other_chip, device_id_type=MESH)
+    for dst in (other_chip, via, onward):
+        pl.semaphore_signal(barrier, 1, device_id=dst, device_id_type=MESH)
 
     load_u = pltpu.make_async_copy(fv, u0.at[pl.ds(1, NJ), pl.ds(1, NI), CELLS], load_sem.at[0])
     load_c = pltpu.make_async_copy(cr, c, load_sem.at[1])
@@ -92,8 +98,9 @@
     pl.when(col == 0)(lambda: zero_i(0))
     pl.when(col == 3)(lambda: zero_i(NI + 1))
 
-    def remote(src, dst, s, n, device):
-        return pltpu.make_async_remote_copy(src, dst, s_sem.at[s, n], r_sem.at[s, n], device_id=device, device_id_type=MESH)
+    def remote(src, dst, s, n, device, n_recv=None):
+        recv = r_sem.at[s, n if n_recv is None else n_recv]
+        return pltpu.make_async_remote_copy(src, dst, s_sem.at[s, n], recv, device_id=device, device_id_type=MESH)
 
     def j_copy(s, way, g):
         start, n = GROUPS[g]
@@ -101,9 +108,37 @@
         a, b = (NJ, 0) if way == UP else (1, NJ + 1)
         return remote(u[s].at[a, rows, CELLS], u[s].at[b, rows, CELLS], s, way + g, to[way])
 
-    def i_copy(s, way):
+    def i_ref(s, half, row):
+        return u[s].at[pl.ds(1 + 4 * half, 4), row, CELLS]
+
+    def i_copy(s, way, half):
         a, b = (NI, 0) if way == I_UP else (1, NI + 1)
-        return remote(u[s].at[pl.ds(1, NJ), a, CELLS], u[s].at[pl.ds(1, NJ), b, CELLS], s, way, to[way])
+        return remote(i_ref(s, half, a), i_ref(s, half, b), s, way + half, to[way])
+
+    def relay_copy(s, way):
+        return remote(i_ref(s, 1, NI if way == I_UP else 1), held.at[s], s, RELAY, via)
+
+    def forward_copy(s, way):
+        return remote(held.at[s], i_ref(s, 1, 0 if way == I_UP else NI + 1), s, FORWARD, onward, way + 1)
+
+    relayed = {I_UP: col == 1, I_DOWN: col == 2}
+    forwards = {I_UP: col == 0, I_DOWN: col == 3}
+    direct = {I_UP: (col == 0) | (col == 2), I_DOWN: (col == 1) | (col == 3)}
+
+    def each_i(s, act):
+        for way in (I_UP, I_DOWN):
+            pl.when(relayed[way])(lambda way=way: act(relay_copy(s, way)))
+        for way in (I_UP, I_DOWN):
+            pl.when(has[way])(lambda way=way: act(i_copy(s, way, 0)))
+            pl.when(direct[way])(lambda way=way: act(i_copy(s, way, 1)))
+
+    def forward(s):
+        for way in (I_UP, I_DOWN):
+
+            @pl.when(forwards[way])
+            def _(way=way):
+                relay_copy(s, way).wait_recv()
+                forward_copy(s, way).start()
 
     def k_copy(s, g):
         start, n = GROUPS[g]
@@ -133,11 +168,7 @@
                     act(j_copy(s, way, g))
 
     def send_i(s):
-        for way in (I_UP, I_DOWN):
-
-            @pl.when(has[way])
-            def _(way=way):
-                i_copy(s, way).start()
+        each_i(s, lambda copy: copy.start())
 
     def send_k(s, gs):
         for g in gs:
@@ -148,7 +179,8 @@
 
             @pl.when(has[back])
             def _(way=way):
-                i_copy(s, way).wait_recv()
+                i_copy(s, way, 0).wait_recv()
+                i_copy(s, way, 1).wait_recv()
 
     def recv_j(s, gs):
         for g in gs:
@@ -185,11 +217,14 @@
     first = jnp.where(r == 0, 0.1, 0.0).astype(F32)
     later = jnp.where(r == 0, 0.0, 0.1).astype(F32)
 
-    def block_totals(groups):
+    k_main = pl.multiple_of(8 * slab, 8)
+    k_edge = pl.multiple_of(NK - 8 - (NK - 8) * slab, 8)
+
+    def block_totals(groups, tiles):
         b = u[2]
 
         def body(i):
-            for k in range(0, NK, 8):
+            for k in tiles:
                 here, lower, upper = pl.ds(K0 + k, 8), pl.ds(K0 + k - 1, 8), pl.ds(K0 + k + 1, 8)
                 own, near = None, None
                 for j in range(1, NJ + 1):
@@ -207,79 +242,83 @@
     def p_copy(n, src, dst, device):
         return pltpu.make_async_remote_copy(src, dst, ps_sem.at[n], pr_sem.at[n], device_id=device, device_id_type=MESH)
 
-    parts = ((4 + 4 * core, 4), (1 + 11 * core, 3), (15 * core, 1))
-    parts_p = ((8 - 4 * core, 4), (12 - 11 * core, 3), (15 - 15 * core, 1))
+    all_k, main, edge = pl.ds(0, NK), pl.ds(k_main, NK - 8), pl.ds(k_edge, 8)
+    main_tiles = [pl.multiple_of(k_main + 8 * t, 8) for t in range(NK // 8 - 1)]
+    pieces = ((1, 13, 2, main), (3, 11, 2, main), (5, 9, 2, main), (7, 8, 1, main), (1, 8, 7, edge), (0, 15, 1, all_k))
+    parts = [(a + (b - a) * core, n, k) for a, b, n, k in pieces]
+    parts_p = [(b + (a - b) * core, n, k) for a, b, n, k in pieces]
+
+    def at(ref, part):
+        start, n, k = part
+        return ref.at[pl.ds(start, n), k]
 
     def t_copy(n):
-        rows = (pl.ds(1, 14), pl.ds(0, 1), pl.ds(15, 1))[n]
-        return p_copy(n, tot.at[rows], tot_p.at[rows], other_core)
+        part = ((1, 2, main), (13, 2, main), (3, 10, main), (1, 14, edge), (0, 1, all_k), (15, 1, all_k))[n]
+        return p_copy(n, at(tot, part), at(tot_p, part), other_core)
 
     def y_copy(n):
-        rows = pl.ds(*parts[n])
-        return p_copy(3 + n, x_out.at[rows], x_in.at[rows], {"rows": r + 4})
+        return p_copy(6 + n, at(x_out, parts[n]), at(x_in, parts[n]), {"rows": r + 4})
 
     def x_copy(n, src):
-        rows = pl.ds(*parts[n])
-        return p_copy(6 + n, src.at[rows], p_in.at[rows], other_chip)
+        return p_copy(6 + CHUNKS + n, at(src, parts[n]), at(p_in, parts[n]), other_chip)
 
     def z_copy(n, mine=True):
-        rows = pl.ds(*(parts if mine else parts_p)[n])
-        return p_copy(9 + n, z.at[rows], z_p.at[rows], other_core)
+        part = (parts if mine else parts_p)[n]
+        return p_copy(6 + 2 * CHUNKS + n, at(z, part), at(z_p, part), other_core)
+
+    def over(part, body):
+        start, n, k = part
+        rows_of(((start, n),), lambda i: body(i, k))
 
     sends_x = ((x_lo == 0), (x_lo == 1) & (y > 0))
     takes_x = (x_lo == 1) | (y > 0)
 
     def chain(n):
-        start, rows = parts[n]
-        own = ((start, rows),)
-
         @pl.when(y > 0)
         def _():
             y_copy(n).wait_recv()
 
-            def body(i):
-                x_out[i] = x_in[i] + (tot[i] + tot_p[i])
-
-            rows_of(own, body)
+            def body(i, k):
+                x_out[i, k, :] = x_in[i, k, :] + (tot[i, k, :] + tot_p[i, k, :])
+
+            over(parts[n], body)
 
         @pl.when(y == 0)
         def _():
-            def body(i):
-                x_out[i] = tot[i] + tot_p[i]
-
-            rows_of(own, body)
+            def body(i, k):
+                x_out[i, k, :] = tot[i, k, :] + tot_p[i, k, :]
+
+            over(parts[n], body)
 
         pl.when(y < 3)(lambda: y_copy(n).start())
         pl.when(sends_x[0])(lambda: x_copy(n, x_out).start())
         pl.when(sends_x[1])(lambda: x_copy(n, x_in).start())
 
     def combine(n):
-        own = (parts[n],)
-
         @pl.when(takes_x)
         def _():
             x_copy(n, x_out).wait_recv()
 
         @pl.when(y > 0)
         def _():
-            def body(i):
-                z[i] = x_in[i] + p_in[i]
-
-            rows_of(own, body)
+            def body(i, k):
+                z[i, k, :] = x_in[i, k, :] + p_in[i, k, :]
+
+            over(parts[n], body)
 
         @pl.when((y == 0) & (x_lo == 1))
         def _():
-            def body(i):
-                z[i] = p_in[i]
-
-            rows_of(own, body)
+            def body(i, k):
+                z[i, k, :] = p_in[i, k, :]
+
+            over(parts[n], body)
 
         @pl.when((y == 0) & (x_lo == 0))
         def _():
-            def body(i):
-                z[i] = zero_plane
-
-            rows_of(own, body)
+            def body(i, k):
+                z[i, k, :] = jnp.zeros((8 if n == 4 else NK if n == 5 else NK - 8, NL), F32)
+
+            over(parts[n], body)
 
         z_copy(n).start()
 
@@ -289,24 +328,28 @@
     take_k(0, ((0, NI),))
     send_k(0, (0, 1, 2))
     each_j(0, (0, 1, 2), lambda copy: copy.start())
+    forward(0)
     load_c.wait()
 
     for s in range(STEPS):
         if s == 2:
+            block_totals(((3, 10),), main_tiles)
+            t_copy(2).start()
+            pl.when(y > 0)(lambda: chain(0))
+            t_copy(2).wait_recv()
+            for n in (1, 2, 3):
+                chain(n)
             recv_k(2, (0, 1, 2))
             put_k(2, ((0, NI),))
-            block_totals(((1, 14),))
-            t_copy(0).start()
-            t_copy(0).wait_recv()
-            chain(0)
-            chain(1)
             recv_i(2)
-            block_totals(((0, 1), (15, 1)))
-            t_copy(1).start()
-            t_copy(2).start()
-            t_copy(1).wait_recv()
-            t_copy(2).wait_recv()
-            chain(2)
+            block_totals(((1, 14),), [k_edge])
+            block_totals(((0, 1), (15, 1)), range(0, NK, 8))
+            for n in (3, 4, 5):
+                t_copy(n).start()
+            for n in (3, 4, 5):
+                t_copy(n).wait_recv()
+            chain(4)
+            chain(5)
         else:
             recv_k(s, (0, 1))
             put_k(s, EDGE)
@@ -318,6 +361,14 @@
             take_k(s + 1, EDGE)
             send_k(s + 1, (0, 1))
             each_j(s + 1, (0, 1), lambda copy: copy.start())
+            forward(s + 1)
+            if s == 1:
+                block_totals(((1, 2), (13, 2)), main_tiles)
+                t_copy(0).start()
+                t_copy(1).start()
+                t_copy(0).wait_recv()
+                t_copy(1).wait_recv()
+                pl.when(y == 0)(lambda: chain(0))
             recv_k(s, (2,))
             put_k(s, MID)
         recv_j(s, (2,))
@@ -327,37 +378,33 @@
             send_k(s + 1, (2,))
             each_j(s + 1, (2,), lambda copy: copy.start())
 
-    for n in range(3):
+    for n in range(CHUNKS):
         combine(n)
 
-    def finish(groups, get):
-        def body(i):
-            below[i] = get(i) + later * (u2[1, i + 1, CELLS, :] - u2[0, i + 1, CELLS, :])
-
-        rows_of(groups, body)
-
-    def finish_part(part, src):
-        pl.when(core == 0)(lambda: finish((part,), lambda i: src[i]))
-        pl.when(core == 1)(lambda: finish((part,), lambda i: src[i] + tot_p[i]))
-
-    for n in range(3):
-        finish_part(parts[n], z)
-    for n in range(3):
+    def finish(part, src):
+        def body(i, k):
+            cells = pl.ds(pl.multiple_of(K0 + k.start, 8), k.size)
+            extra = later * (u2[1, i + 1, cells, :] - u2[0, i + 1, cells, :])
+            below[i, k, :] = src[i, k, :] + (extra + jnp.where(core == 1, tot_p[i, k, :], 0.0))
+
+        over(part, body)
+
+    for n in range(CHUNKS):
+        finish(parts[n], z)
+    for n in range(CHUNKS):
         z_copy(n, mine=False).wait_recv()
-        finish_part(parts_p[n], z_p)
+        finish(parts_p[n], z_p)
 
     for s in range(STEPS):
         each_j(s, (0, 1, 2), lambda copy: copy.wait_send())
+        each_i(s, lambda copy: copy.wait_send())
         for way in (I_UP, I_DOWN):
-
-            @pl.when(has[way])
-            def _(way=way, s=s):
-                i_copy(s, way).wait_send()
-
+            pl.when(forwards[way])(lambda way=way, s=s: forward_copy(s, way).wait_send())
         for g in range(3):
             k_copy(s, g).wait_send()
-    for n in range(3):
+    for n in range(6):
         t_copy(n).wait_send()
+    for n in range(CHUNKS):
         z_copy(n).wait_send()
         pl.when(y < 3)(lambda n=n: y_copy(n).wait_send())
         pl.when(sends_x[0] | sends_x[1])(lambda n=n: x_copy(n, x_out).wait_send())
@@ -401,9 +448,10 @@
         scratch_shapes=[pltpu.VMEM(padded, F32)] * 3
         + [pltpu.VMEM(block, F32)]
         + [pltpu.VMEM((STEPS, NI, NJ, NL), F32)] * 2
+        + [pltpu.VMEM((STEPS, 4, NK, NL), F32)]
         + [pltpu.VMEM(plane, F32)] * 7
-        + [sems((2,)), sems((STEPS, N_SEM)), sems((STEPS, N_SEM)), sems((12,)), sems((12,))],
-        compiler_params=pltpu.CompilerParams(collective_id=1, has_side_effects=True, vmem_limit_bytes=44 * 2**20),
+        + [sems((2,)), sems((STEPS, N_SEM)), sems((STEPS, N_SEM)), sems((6 + 3 * CHUNKS,)), sems((6 + 3 * CHUNKS,))],
+        compiler_params=pltpu.CompilerParams(collective_id=1, has_side_effects=True, vmem_limit_bytes=57 * 2**20),
         name="exchange",
     )(field_values, crowding)
     full = jax.ShapeDtypeStruct(block, F32)

time: 95.3 us -> 81.7 us (0.86)
  Pallas kernels: 92.4 us -> 80.4 us
  local copies, waits for them, and re-layouts: 2.18 us -> 0 us
    pallas_call x1, Pallas kernels: 89 us -> 77 us  [on_device(): pl.pallas_call(exchange_kernel, out_shape=(pltpu.VMEM(block, F32), pltpu....]
    unnamed x2 -> x0, local copies, waits for them, and re-layouts: 2.18 us -> none
where the time goes in v2:
time: 81.7 us; the launch traced here: 81 us
  Pallas kernels  80.4 us (98%)
    pallas_call x1, Pallas kernels, on_device(): pl.pallas_call(exchange_kernel, out_shape=(pltpu.VMEM(block, F32), pltpu....  77 us
    pallas_call x1, Pallas kernels, on_device(): pl.pallas_call(write_kernel, out_shape=(full, full), in_specs=[vmem, vmem...  3.34 us

profile of v2, /device:TPU:59, one launch (start us, length us, event | category | flops | bytes accessed | tf_op | source)
XLA Modules:
  0.0 81.0 jit_solution(940831442879512680)
XLA Ops:
  0.6 77.0 %exchange.1 = (f32[8,16,64,128]{3,2,1,0:T(8,128)S(1)}, f32[16,64,128]{2,1,0:T(8,128)S(1)}) custom-call(f32[8,16,64,128]{3,2,1,0:T(8,128)} %fv.1, f32[8,16,64,128]{3,2,1,0:T(8,128)} %cr.1), custom_call_target="tpu_custom_call" | custom-call | tf_op jit(solution)/shard_map/exchange/pallas_call | solution.py:443
  77.7 3.3 %write.1 = (f32[8,16,64,128]{3,2,1,0:T(8,128)}, f32[8,16,64,128]{3,2,1,0:T(8,128)}) custom-call(f32[8,16,64,128]{3,2,1,0:T(8,128)S(1)} %get-tuple-element.4.v, f32[16,64,128]{2,1,0:T(8,128)S(1)} %get-tuple-element.5.below), custom_call_target="tpu_custom_call" | custom-call | tf_op jit(solution)/shard_map/write/pallas_call | solution.py:458

commit v3 on v2

--- a/solution.py
+++ b/solution.py
@@ -12,15 +12,14 @@
 STEPS = 3
 NJ, NI, NK, NL = 8, 16, 64, 128
 K0 = 8
-EDGE = ((0, 4), (12, 4))
-MID = ((4, 8),)
-GROUPS = EDGE + MID
+PIECES = ((0, 1), (15, 1), (1, 4), (11, 4), (5, 4), (9, 2))
+WAVES = ((0, 1), (2, 3), (4, 5))
+DETOUR = (2, 4, 3)
 CELLS = pl.ds(K0, NK)
-N_SEM = 15
-UP, DOWN, I_UP, I_DOWN, KF, RELAY, FORWARD = 0, 3, 6, 8, 10, 13, 14
-
-
-CHUNKS = 6
+N_SEM = 30
+UP, DOWN, I_UP, I_DOWN, KF, RELAY, FORWARD, J_RELAY, J_FORWARD = 0, 6, 12, 14, 16, 22, 23, 24, 27
+
+CHUNKS = 5
 
 
 def rows_of(groups, body):
@@ -28,7 +27,7 @@
         lax.fori_loop(start, start + count, lambda i, _: (body(i), 0)[1], 0)
 
 
-def exchange_kernel(fv, cr, out, below, u0, u1, u2, c, kf, kh, held, tot, tot_p, x_in, x_out, p_in, z, z_p, load_sem, s_sem, r_sem, ps_sem, pr_sem):
+def exchange_kernel(fv, cr, out, below, u0, u1, u2, c, kf, kh, held, held_j, tot, tot_p, x_in, x_out, p_in, z, z_p, load_sem, go_sem, s_sem, r_sem, ps_sem, pr_sem):
     r, col, slab = lax.axis_index("rows"), lax.axis_index("cols"), lax.axis_index("slabs")
     core = lax.rem(r, 2)
     x_lo = lax.rem(lax.div(r, 2), 2)
@@ -41,25 +40,32 @@
 
     has = {UP: r < 15, DOWN: r > 0, I_UP: col < 3, I_DOWN: col > 0}
     to = {UP: {"rows": r + 1}, DOWN: {"rows": r - 1}, I_UP: {"cols": col + 1}, I_DOWN: {"cols": col - 1}}
+    top, bottom = lax.rem(r, 4) == 3, lax.rem(r, 4) == 0
+    across = {"rows": jnp.where(top, r - 3, r + 3)}
+    over_slab = {"slabs": 1 - slab}
+    near_col = {"cols": col + 1 - 2 * lax.rem(col, 2)}
+    yes = r >= 0
+    greets = (
+        (has[UP], to[UP], has[UP]),
+        (has[DOWN], to[DOWN], has[DOWN]),
+        (y < 3, {"rows": r + 4}, y < 3),
+        (y > 0, {"rows": r - 4}, y > 0),
+        (top | bottom, across, top | bottom),
+        (yes, other_chip, yes),
+        (yes, near_col, yes),
+        (yes, via, yes),
+        (slab == 0, over_slab, slab == 1),
+        (col == 1, to[I_UP], col == 2),
+        (col < 2, onward, col > 1),
+    )
     barrier = pltpu.get_barrier_semaphore()
-    count = jnp.int32(4)
-    for way in (UP, DOWN, I_UP, I_DOWN):
-        count = count + jnp.where(has[way], 1, 0)
-
-        @pl.when(has[way])
-        def _(way=way):
-            pl.semaphore_signal(barrier, 1, device_id=to[way], device_id_type=MESH)
-
-    for ok, dst in ((y < 3, {"rows": r + 4}), (y > 0, {"rows": r - 4})):
-        count = count + jnp.where(ok, 1, 0)
-
-        @pl.when(ok)
+    count = jnp.int32(0)
+    for signals, dst, signalled in greets:
+        count = count + jnp.where(signalled, 1, 0)
+
+        @pl.when(signals)
         def _(dst=dst):
             pl.semaphore_signal(barrier, 1, device_id=dst, device_id_type=MESH)
-
-    pl.semaphore_signal(barrier, 1, device_id={"slabs": 1 - slab}, device_id_type=MESH)
-    for dst in (other_chip, via, onward):
-        pl.semaphore_signal(barrier, 1, device_id=dst, device_id_type=MESH)
 
     load_u = pltpu.make_async_copy(fv, u0.at[pl.ds(1, NJ), pl.ds(1, NI), CELLS], load_sem.at[0])
     load_c = pltpu.make_async_copy(cr, c, load_sem.at[1])
@@ -102,11 +108,31 @@
         recv = r_sem.at[s, n if n_recv is None else n_recv]
         return pltpu.make_async_remote_copy(src, dst, s_sem.at[s, n], recv, device_id=device, device_id_type=MESH)
 
+    def j_ref(s, g, plane):
+        start, n = PIECES[g]
+        return u[s].at[plane, pl.ds(start + 1, n), CELLS]
+
     def j_copy(s, way, g):
-        start, n = GROUPS[g]
-        rows = pl.ds(start + 1, n)
         a, b = (NJ, 0) if way == UP else (1, NJ + 1)
-        return remote(u[s].at[a, rows, CELLS], u[s].at[b, rows, CELLS], s, way + g, to[way])
+        return remote(j_ref(s, g, a), j_ref(s, g, b), s, way + g, to[way])
+
+    def j_relay(s, way, g):
+        n = DETOUR.index(g)
+        far = {"rows": r + 4 if way == UP else r - 4}
+        return remote(j_ref(s, g, NJ if way == UP else 1), held_j.at[s, n], s, J_RELAY + n, far)
+
+    def j_onward(s, way, g):
+        n = DETOUR.index(g)
+        return remote(held_j.at[s, n], j_ref(s, g, 0 if way == UP else NJ + 1), s, J_FORWARD + n, across, way + g)
+
+    detours = {
+        UP: {2: top & (y < 3), 4: top & (y < 3) & (y > 0), 3: top & (y == 2)},
+        DOWN: {2: bottom & (y > 0), 4: bottom & (y > 0) & (y < 3), 3: bottom & (y == 1)},
+    }
+    passes = {
+        UP: {2: top & (y > 0), 4: top & (y > 1), 3: top & (y == 3)},
+        DOWN: {2: bottom & (y < 3), 4: bottom & (y < 2), 3: bottom & (y == 0)},
+    }
 
     def i_ref(s, half, row):
         return u[s].at[pl.ds(1 + 4 * half, 4), row, CELLS]
@@ -125,12 +151,17 @@
     forwards = {I_UP: col == 0, I_DOWN: col == 3}
     direct = {I_UP: (col == 0) | (col == 2), I_DOWN: (col == 1) | (col == 3)}
 
-    def each_i(s, act):
+    far = {I_UP: col == 1, I_DOWN: col == 2}
+
+    def each_i(s, act, near=True, beyond=True):
+        if near:
+            for way in (I_UP, I_DOWN):
+                pl.when(relayed[way])(lambda way=way: act(relay_copy(s, way)))
         for way in (I_UP, I_DOWN):
-            pl.when(relayed[way])(lambda way=way: act(relay_copy(s, way)))
-        for way in (I_UP, I_DOWN):
-            pl.when(has[way])(lambda way=way: act(i_copy(s, way, 0)))
-            pl.when(direct[way])(lambda way=way: act(i_copy(s, way, 1)))
+            if near:
+                pl.when(direct[way])(lambda way=way: [act(i_copy(s, way, half)) for half in (0, 1)] and None)
+            if beyond:
+                pl.when(far[way])(lambda way=way: act(i_copy(s, way, 0)))
 
     def forward(s):
         for way in (I_UP, I_DOWN):
@@ -141,7 +172,7 @@
                 forward_copy(s, way).start()
 
     def k_copy(s, g):
-        start, n = GROUPS[g]
+        start, n = PIECES[g]
         rows = pl.ds(start, n)
         return remote(kf.at[s, rows], kh.at[s, rows], s, KF + g, {"slabs": 1 - slab})
 
@@ -162,13 +193,23 @@
     def each_j(s, gs, act):
         for g in gs:
             for way in (UP, DOWN):
-
-                @pl.when(has[way])
+                straight = has[way]
+                if g in DETOUR:
+                    straight = straight & jnp.logical_not(detours[way][g])
+                    pl.when(detours[way][g])(lambda way=way, g=g: act(j_relay(s, way, g)))
+                pl.when(straight)(lambda way=way, g=g: act(j_copy(s, way, g)))
+
+    def pass_j(s, gs):
+        for g in gs:
+            for way in (UP, DOWN):
+
+                @pl.when(passes[way][g])
                 def _(way=way, g=g):
-                    act(j_copy(s, way, g))
-
-    def send_i(s):
-        each_i(s, lambda copy: copy.start())
+                    j_relay(s, way, g).wait_recv()
+                    j_onward(s, way, g).start()
+
+    def send_i(s, **which):
+        each_i(s, lambda copy: copy.start(), **which)
 
     def send_k(s, gs):
         for g in gs:
@@ -244,7 +285,7 @@
 
     all_k, main, edge = pl.ds(0, NK), pl.ds(k_main, NK - 8), pl.ds(k_edge, 8)
     main_tiles = [pl.multiple_of(k_main + 8 * t, 8) for t in range(NK // 8 - 1)]
-    pieces = ((1, 13, 2, main), (3, 11, 2, main), (5, 9, 2, main), (7, 8, 1, main), (1, 8, 7, edge), (0, 15, 1, all_k))
+    pieces = ((1, 12, 3, main), (4, 10, 2, main), (6, 8, 2, main), (1, 8, 7, edge), (0, 15, 1, all_k))
     parts = [(a + (b - a) * core, n, k) for a, b, n, k in pieces]
     parts_p = [(b + (a - b) * core, n, k) for a, b, n, k in pieces]
 
@@ -253,7 +294,7 @@
         return ref.at[pl.ds(start, n), k]
 
     def t_copy(n):
-        part = ((1, 2, main), (13, 2, main), (3, 10, main), (1, 14, edge), (0, 1, all_k), (15, 1, all_k))[n]
+        part = ((1, 3, main), (12, 3, main), (4, 8, main), (1, 14, edge), (0, 1, all_k), (15, 1, all_k))[n]
         return p_copy(n, at(tot, part), at(tot_p, part), other_core)
 
     def y_copy(n):
@@ -316,67 +357,91 @@
         @pl.when((y == 0) & (x_lo == 0))
         def _():
             def body(i, k):
-                z[i, k, :] = jnp.zeros((8 if n == 4 else NK if n == 5 else NK - 8, NL), F32)
+                z[i, k, :] = jnp.zeros((8 if n == 3 else NK if n == 4 else NK - 8, NL), F32)
 
             over(parts[n], body)
 
         z_copy(n).start()
 
     pl.semaphore_wait(barrier, count)
+
+    @pl.when(slab == 1)
+    def _():
+        pl.semaphore_signal(go_sem.at[0], 1, device_id=over_slab, device_id_type=MESH)
+
+    @pl.when(col == 2)
+    def _():
+        pl.semaphore_signal(go_sem.at[1], 1, device_id=to[I_DOWN], device_id_type=MESH)
+        pl.semaphore_signal(go_sem.at[1], 1, device_id=onward, device_id_type=MESH)
+
     load_u.wait()
-    send_i(0)
+    send_i(0, beyond=False)
+    each_j(0, WAVES[0], lambda copy: copy.start())
     take_k(0, ((0, NI),))
-    send_k(0, (0, 1, 2))
-    each_j(0, (0, 1, 2), lambda copy: copy.start())
+    pl.when(col < 2)(lambda: pl.semaphore_wait(go_sem.at[1], 1))
+    send_i(0, near=False)
     forward(0)
+    pl.when(slab == 0)(lambda: pl.semaphore_wait(go_sem.at[0], 1))
+    for wave in WAVES:
+        send_k(0, wave)
+    each_j(0, WAVES[1], lambda copy: copy.start())
+    pass_j(0, (2, 3))
+    each_j(0, WAVES[2], lambda copy: copy.start())
+    pass_j(0, (4,))
     load_c.wait()
 
     for s in range(STEPS):
         if s == 2:
-            block_totals(((3, 10),), main_tiles)
+            block_totals(((4, 8),), main_tiles)
             t_copy(2).start()
             pl.when(y > 0)(lambda: chain(0))
             t_copy(2).wait_recv()
-            for n in (1, 2, 3):
-                chain(n)
-            recv_k(2, (0, 1, 2))
-            put_k(2, ((0, NI),))
+            pass_j(2, (4,))
+            chain(1)
+            chain(2)
+            for wave in WAVES:
+                recv_k(2, wave)
+            put_k(2, PIECES)
+            block_totals(((1, 14),), [k_edge])
+            t_copy(3).start()
+            t_copy(3).wait_recv()
+            chain(3)
             recv_i(2)
-            block_totals(((1, 14),), [k_edge])
             block_totals(((0, 1), (15, 1)), range(0, NK, 8))
-            for n in (3, 4, 5):
+            for n in (4, 5):
                 t_copy(n).start()
-            for n in (3, 4, 5):
+            for n in (4, 5):
                 t_copy(n).wait_recv()
             chain(4)
-            chain(5)
-        else:
-            recv_k(s, (0, 1))
-            put_k(s, EDGE)
-            recv_i(s)
-        recv_j(s, (0, 1))
-        march(s, EDGE)
-        if s < 2:
-            send_i(s + 1)
-            take_k(s + 1, EDGE)
-            send_k(s + 1, (0, 1))
-            each_j(s + 1, (0, 1), lambda copy: copy.start())
-            forward(s + 1)
-            if s == 1:
-                block_totals(((1, 2), (13, 2)), main_tiles)
-                t_copy(0).start()
-                t_copy(1).start()
-                t_copy(0).wait_recv()
-                t_copy(1).wait_recv()
-                pl.when(y == 0)(lambda: chain(0))
-            recv_k(s, (2,))
-            put_k(s, MID)
-        recv_j(s, (2,))
-        march(s, MID)
-        if s < 2:
-            take_k(s + 1, MID)
-            send_k(s + 1, (2,))
-            each_j(s + 1, (2,), lambda copy: copy.start())
+        for n, wave in enumerate(WAVES):
+            rows = [PIECES[g] for g in wave]
+            if s < 2:
+                recv_k(s, wave)
+                put_k(s, rows)
+                if n == 0:
+                    recv_i(s)
+            recv_j(s, wave)
+            if s == 1 and n == 0:
+                pass_j(1, (4,))
+            march(s, rows)
+            if s < 2:
+                if n == 0:
+                    send_i(s + 1)
+                take_k(s + 1, rows)
+                send_k(s + 1, wave)
+                each_j(s + 1, wave, lambda copy: copy.start())
+                if n == 1:
+                    forward(s + 1)
+                    if s == 1:
+                        block_totals(((1, 3), (12, 3)), main_tiles)
+                        t_copy(0).start()
+                        t_copy(1).start()
+                    if s == 1:
+                        t_copy(0).wait_recv()
+                        t_copy(1).wait_recv()
+                        pl.when(y == 0)(lambda: chain(0))
+                elif n == 2:
+                    pass_j(s + 1, (2, 3))
 
     for n in range(CHUNKS):
         combine(n)
@@ -396,11 +461,14 @@
         finish(parts_p[n], z_p)
 
     for s in range(STEPS):
-        each_j(s, (0, 1, 2), lambda copy: copy.wait_send())
+        each_j(s, range(6), lambda copy: copy.wait_send())
+        for g in DETOUR:
+            for way in (UP, DOWN):
+                pl.when(passes[way][g])(lambda way=way, g=g, s=s: j_onward(s, way, g).wait_send())
         each_i(s, lambda copy: copy.wait_send())
         for way in (I_UP, I_DOWN):
             pl.when(forwards[way])(lambda way=way, s=s: forward_copy(s, way).wait_send())
-        for g in range(3):
+        for g in range(6):
             k_copy(s, g).wait_send()
     for n in range(6):
         t_copy(n).wait_send()
@@ -448,9 +516,9 @@
         scratch_shapes=[pltpu.VMEM(padded, F32)] * 3
         + [pltpu.VMEM(block, F32)]
         + [pltpu.VMEM((STEPS, NI, NJ, NL), F32)] * 2
-        + [pltpu.VMEM((STEPS, 4, NK, NL), F32)]
+        + [pltpu.VMEM((STEPS, 4, NK, NL), F32), pltpu.VMEM((STEPS, len(DETOUR), 4, NK, NL), F32)]
         + [pltpu.VMEM(plane, F32)] * 7
-        + [sems((2,)), sems((STEPS, N_SEM)), sems((STEPS, N_SEM)), sems((6 + 3 * CHUNKS,)), sems((6 + 3 * CHUNKS,))],
+        + [sems((2,)), pltpu.SemaphoreType.REGULAR((2,)), sems((STEPS, N_SEM)), sems((STEPS, N_SEM)), sems((6 + 3 * CHUNKS,)), sems((6 + 3 * CHUNKS,))],
         compiler_params=pltpu.CompilerParams(collective_id=1, has_side_effects=True, vmem_limit_bytes=57 * 2**20),
         name="exchange",
     )(field_values, crowding)

time: 81.7 us -> 78.8 us (0.965)
  Pallas kernels: 80.4 us -> 76.8 us
    pallas_call x1, Pallas kernels: 77 us -> 73.5 us  [on_device(): pl.pallas_call(exchange_kernel, out_shape=(pltpu.VMEM(block, F32), pltpu....]
where the time goes in v3:
time: 78.8 us; the launch traced here: 77.5 us
  Pallas kernels  76.8 us (97%)
    pallas_call x1, Pallas kernels, on_device(): pl.pallas_call(exchange_kernel, out_shape=(pltpu.VMEM(block, F32), pltpu....  73.5 us
    pallas_call x1, Pallas kernels, on_device(): pl.pallas_call(write_kernel, out_shape=(full, full), in_specs=[vmem, vmem...  3.34 us

profile of v3, /device:TPU:59, one launch (start us, length us, event | category | flops | bytes accessed | tf_op | source)
XLA Modules:
  0.0 77.5 jit_solution(3435465405710096389)
XLA Ops:
  0.6 73.5 %exchange.1 = (f32[8,16,64,128]{3,2,1,0:T(8,128)S(1)}, f32[16,64,128]{2,1,0:T(8,128)S(1)}) custom-call(f32[8,16,64,128]{3,2,1,0:T(8,128)} %fv.1, f32[8,16,64,128]{3,2,1,0:T(8,128)} %cr.1), custom_call_target="tpu_custom_call" | custom-call | tf_op jit(solution)/shard_map/exchange/pallas_call | solution.py:511
  74.1 3.3 %write.1 = (f32[8,16,64,128]{3,2,1,0:T(8,128)}, f32[8,16,64,128]{3,2,1,0:T(8,128)}) custom-call(f32[8,16,64,128]{3,2,1,0:T(8,128)S(1)} %get-tuple-element.4.v, f32[16,64,128]{2,1,0:T(8,128)S(1)} %get-tuple-element.5.below), custom_call_target="tpu_custom_call" | custom-call | tf_op jit(solution)/shard_map/write/pallas_call | solution.py:526

commit v4 on v3

--- a/solution.py
+++ b/solution.py
@@ -27,7 +27,7 @@
         lax.fori_loop(start, start + count, lambda i, _: (body(i), 0)[1], 0)
 
 
-def exchange_kernel(fv, cr, out, below, u0, u1, u2, c, kf, kh, held, held_j, tot, tot_p, x_in, x_out, p_in, z, z_p, load_sem, go_sem, s_sem, r_sem, ps_sem, pr_sem):
+def exchange_kernel(fv, cr, out, below, u0, u1, u2, c, kf, kh, held, held_j, tot, tot_p, x_in, x_out, p_in, z, z_p, chip, from_y, load_sem, go_sem, s_sem, r_sem, ps_sem, pr_sem):
     r, col, slab = lax.axis_index("rows"), lax.axis_index("cols"), lax.axis_index("slabs")
     core = lax.rem(r, 2)
     x_lo = lax.rem(lax.div(r, 2), 2)
@@ -50,6 +50,10 @@
         (has[DOWN], to[DOWN], has[DOWN]),
         (y < 3, {"rows": r + 4}, y < 3),
         (y > 0, {"rows": r - 4}, y > 0),
+        (y < 2, {"rows": r + 8}, y < 2),
+        (y > 1, {"rows": r - 8}, y > 1),
+        (y < 1, {"rows": r + 12}, y < 1),
+        (y > 2, {"rows": r - 12}, y > 2),
         (top | bottom, across, top | bottom),
         (yes, other_chip, yes),
         (yes, near_col, yes),
@@ -300,6 +304,9 @@
     def y_copy(n):
         return p_copy(6 + n, at(x_out, parts[n]), at(x_in, parts[n]), {"rows": r + 4})
 
+    def far_copy(n, d):
+        return p_copy(6 + 3 * CHUNKS + 3 * (n - 3) + d - 1, at(chip, parts[n]), at(from_y.at[d - 1], parts[n]), {"rows": r + 4 * d})
+
     def x_copy(n, src):
         return p_copy(6 + CHUNKS + n, at(src, parts[n]), at(p_in, parts[n]), other_chip)
 
@@ -332,8 +339,42 @@
             over(parts[n], body)
 
         pl.when(y < 3)(lambda: y_copy(n).start())
+        pair_sends(n)
+
+    def pair_sends(n):
         pl.when(sends_x[0])(lambda: x_copy(n, x_out).start())
         pl.when(sends_x[1])(lambda: x_copy(n, x_in).start())
+
+    def spread(n):
+        def body(i, k):
+            chip[i, k, :] = tot[i, k, :] + tot_p[i, k, :]
+
+        over(parts[n], body)
+        for d in (1, 2, 3):
+            pl.when(y + d < 4)(lambda d=d: far_copy(n, d).start())
+
+    def gather(n):
+        for d in (1, 2, 3):
+
+            @pl.when(y >= d)
+            def _(d=d):
+                far_copy(n, d).wait_recv()
+
+                def body(i, k):
+                    x_in[i, k, :] = from_y[0, i, k, :] if d == 1 else x_in[i, k, :] + from_y[d - 1, i, k, :]
+
+                over(parts[n], body)
+
+        def body(i, k):
+            x_out[i, k, :] = chip[i, k, :] + x_in[i, k, :]
+
+        pl.when(y > 0)(lambda: over(parts[n], body))
+
+        def alone(i, k):
+            x_out[i, k, :] = chip[i, k, :]
+
+        pl.when(y == 0)(lambda: over(parts[n], alone))
+        pair_sends(n)
 
     def combine(n):
         @pl.when(takes_x)
@@ -405,14 +446,16 @@
             block_totals(((1, 14),), [k_edge])
             t_copy(3).start()
             t_copy(3).wait_recv()
-            chain(3)
+            spread(3)
             recv_i(2)
             block_totals(((0, 1), (15, 1)), range(0, NK, 8))
             for n in (4, 5):
                 t_copy(n).start()
             for n in (4, 5):
                 t_copy(n).wait_recv()
-            chain(4)
+            spread(4)
+            gather(3)
+            gather(4)
         for n, wave in enumerate(WAVES):
             rows = [PIECES[g] for g in wave]
             if s < 2:
@@ -474,7 +517,11 @@
         t_copy(n).wait_send()
     for n in range(CHUNKS):
         z_copy(n).wait_send()
-        pl.when(y < 3)(lambda n=n: y_copy(n).wait_send())
+        if n < 3:
+            pl.when(y < 3)(lambda n=n: y_copy(n).wait_send())
+        else:
+            for d in (1, 2, 3):
+                pl.when(y + d < 4)(lambda n=n, d=d: far_copy(n, d).wait_send())
         pl.when(sends_x[0] | sends_x[1])(lambda n=n: x_copy(n, x_out).wait_send())
 
 
@@ -517,8 +564,9 @@
         + [pltpu.VMEM(block, F32)]
         + [pltpu.VMEM((STEPS, NI, NJ, NL), F32)] * 2
         + [pltpu.VMEM((STEPS, 4, NK, NL), F32), pltpu.VMEM((STEPS, len(DETOUR), 4, NK, NL), F32)]
-        + [pltpu.VMEM(plane, F32)] * 7
-        + [sems((2,)), pltpu.SemaphoreType.REGULAR((2,)), sems((STEPS, N_SEM)), sems((STEPS, N_SEM)), sems((6 + 3 * CHUNKS,)), sems((6 + 3 * CHUNKS,))],
+        + [pltpu.VMEM(plane, F32)] * 8
+        + [pltpu.VMEM((3,) + plane, F32)]
+        + [sems((2,)), pltpu.SemaphoreType.REGULAR((2,)), sems((STEPS, N_SEM)), sems((STEPS, N_SEM)), sems((12 + 3 * CHUNKS,)), sems((12 + 3 * CHUNKS,))],
         compiler_params=pltpu.CompilerParams(collective_id=1, has_side_effects=True, vmem_limit_bytes=57 * 2**20),
         name="exchange",
     )(field_values, crowding)

time: 78.8 us -> 77.4 us (0.982); the launches traced: 77.5 us -> 77.1 us
  no operation moved by 1% of the time
where the time goes in v4:
time: 77.4 us; the launch traced here: 77.1 us
  Pallas kernels  76.5 us (99%)
    pallas_call x1, Pallas kernels, on_device(): pl.pallas_call(exchange_kernel, out_shape=(pltpu.VMEM(block, F32), pltpu....  73.1 us
    pallas_call x1, Pallas kernels, on_device(): pl.pallas_call(write_kernel, out_shape=(full, full), in_specs=[vmem, vmem...  3.34 us

profile of v4, /device:TPU:59, one launch (start us, length us, event | category | flops | bytes accessed | tf_op | source)
XLA Modules:
  0.0 77.1 jit_solution(11574846821267845836)
XLA Ops:
  0.6 73.1 %exchange.1 = (f32[8,16,64,128]{3,2,1,0:T(8,128)S(1)}, f32[16,64,128]{2,1,0:T(8,128)S(1)}) custom-call(f32[8,16,64,128]{3,2,1,0:T(8,128)} %fv.1, f32[8,16,64,128]{3,2,1,0:T(8,128)} %cr.1), custom_call_target="tpu_custom_call" | custom-call | tf_op jit(solution)/shard_map/exchange/pallas_call | solution.py:558
  73.7 3.3 %write.1 = (f32[8,16,64,128]{3,2,1,0:T(8,128)}, f32[8,16,64,128]{3,2,1,0:T(8,128)}) custom-call(f32[8,16,64,128]{3,2,1,0:T(8,128)S(1)} %get-tuple-element.4.v, f32[16,64,128]{2,1,0:T(8,128)S(1)} %get-tuple-element.5.below), custom_call_target="tpu_custom_call" | custom-call | tf_op jit(solution)/shard_map/write/pallas_call | solution.py:574
